TPU v7x, 32 devices: a whole 2x2x4 slice. The times are simulated.
32 devices in a mesh: rep: 2 (over y), seq: 4 (over z), head: 2 (over x), sub: 2 (over core).
Axes of the slice: x: 2, y: 2, z: 4, core: 2. Of those that a mesh axis runs over, the one named last changes fastest.
Arguments:
- tokens: bfloat16 [32, 4096], P(('rep', 'sub'), 'seq'), parts along dimension 0, may hold values from -260 to 260
- attn_gain: float32 [4096], P('seq'), may hold values from 0.1 to 1.9
- w_query: bfloat16 [4096, 4096], P('seq', 'head'), may hold values from -0.09375 to 0.09375
- key_projection_weight: bfloat16 [4096, 1024], P('seq', 'head'), may hold values from -0.375 to 0.375
- value_projection_weight: bfloat16 [4096, 1024], P('seq', 'head'), may hold values from -0.375 to 0.375
- w_attn_out: bfloat16 [4096, 4096], P('head', 'seq'), may hold values from -0.09375 to 0.09375
- cache_keys: bfloat16 [32, 8, 2048, 128], P(('rep', 'sub'), 'head', 'seq'), parts along dimension 0, may hold values from -2500 to 2500
- stored_value_cache: bfloat16 [32, 8, 2048, 128], P(('rep', 'sub'), 'head', 'seq'), parts along dimension 0, may hold values from -12 to 12
- lengths: int32 [32], P(('rep', 'sub')), parts along dimension 0, may hold values from 1024 to 2048
- positions: int32 [32], P(('rep', 'sub')), parts along dimension 0, may hold values from 0 to 2047
- mamba_gain: float32 [4096], replicated, may hold values from 0.1 to 1.9
- w_in: bfloat16 [2, 4096, 8192], P(None, None, ('seq', 'head')), may hold values from -0.09375 to 0.09375
- conv_weight: float32 [4, 8192], P(None, ('seq', 'head')), may hold values from -3 to 3
- conv_bias: float32 [8192], P(('seq', 'head')), may hold values from -0.5 to 0.5
- conv_state: float32 [32, 3, 8192], P(('rep', 'sub'), None, ('seq', 'head')), parts along dimension 0, may hold values from -6 to 6
- w_xproj: bfloat16 [8192, 288], P(('seq', 'head')), may hold values from -0.0625 to 0.0625
- w_dt: bfloat16 [256, 8192], P(None, ('seq', 'head')), may hold values from -0.375 to 0.375
- dt_bias: float32 [8192], P(('seq', 'head')), may hold values from -4 to 0
- a_log: float32 [16, 8192], P(None, ('seq', 'head')), may hold values from 0 to 2.77
- skip_gain: float32 [8192], P(('seq', 'head')), may hold values from 0.25 to 2
- ssm_state: float32 [32, 16, 8192], P(('rep', 'sub'), None, ('seq', 'head')), parts along dimension 0, may hold values from -6 to 6
- w_mamba_out: bfloat16 [8192, 4096], P(('seq', 'head')), may hold values from -0.09375 to 0.09375
Outputs:
- hidden_out: bfloat16 [32, 4096], P(('rep', 'sub'), 'seq'), parts along dimension 0
- new_state: float32 [32, 16, 8192], P(('rep', 'sub'), None, ('seq', 'head')), parts along dimension 0
There are 2 independent parts, one for each index of `rep`. A program takes and returns all parts, laid end to end along the dimension named above; an argument that names none is the same for every part. Nothing has to cross between parts.
Inputs may be any that keep to these rules, and one draw needn't show every extreme that they name: Cache positions p < lengths[b] hold sequence b's past keys and values; later positions are not attended.
All inputs are finite; a program needn't handle non-finite values.
Results may differ from a plain program's by a relative error of at most 0.015.
Values may be sent and summed in bfloat16 or wider, within the bound.
A program may use at most 128 MiB of HBM per device.

v0:
```python
import math
import jax
import jax.numpy as jnp
from jax import lax
from jax.sharding import PartitionSpec as P

norm_eps = 1e-05
masked_floor = -1e30
rope_base = 10000.0


def joined(value, axis, join):
    pieces = jax.tree.map(lambda part: lax.all_gather(part, axis), value)
    head = jax.tree.map(lambda part: part[0], pieces)
    tail = jax.tree.map(lambda part: part[1:], pieces)
    subtotal, _ = lax.scan(lambda subtotal, section: (join(subtotal, section), None), head, tail)
    return subtotal


def apply_rotary(vectors, positions):
    half_dim = vectors.shape[-1] // 2
    frequency = jnp.exp(
        -math.log(rope_base) * 2.0 * jnp.arange(half_dim, dtype=jnp.float32) / (2 * half_dim)
    )
    angles = positions.astype(jnp.float32)[:, None] * frequency[None, :]
    cosine = jnp.cos(angles)[:, None, :]
    sine_part = jnp.sin(angles)[:, None, :]
    first_half = vectors[..., :half_dim]
    second_half = vectors[..., half_dim:]
    return jnp.concatenate(
        [
            first_half * cosine - second_half * sine_part,
            second_half * cosine + first_half * sine_part,
        ],
        axis=-1,
    )


def join_partial(earlier, later):
    max_one, sum_one, acc_one = earlier
    max_two, sum_two, acc_two = later
    joined_max = jnp.maximum(max_one, max_two)
    factor_one = jnp.exp(max_one - joined_max)
    factor_two = jnp.exp(max_two - joined_max)
    return (
        joined_max,
        sum_one * factor_one + sum_two * factor_two,
        acc_one * factor_one[..., None] + acc_two * factor_two[..., None],
    )


def local(
    tokens,
    attn_gain,
    w_query,
    key_projection_weight,
    value_projection_weight,
    w_attn_out,
    cache_keys,
    stored_value_cache,
    lengths,
    positions,
    mamba_gain,
    w_in,
    conv_weight,
    conv_bias,
    conv_state,
    w_xproj,
    w_dt,
    dt_bias,
    a_log,
    skip_gain,
    ssm_state,
    w_mamba_out,
):
    batch_rows = tokens.shape[0]
    feature_cols = tokens.shape[1]
    head_dim = cache_keys.shape[3]
    kv_local = cache_keys.shape[1]
    ctx_local = cache_keys.shape[2]
    q_local = w_query.shape[1] // head_dim
    query_group_count = q_local // kv_local
    model_width = feature_cols * lax.axis_size("seq")
    token_float = tokens.astype(jnp.float32)
    lifted = (token_float * attn_gain[None, :]).astype(jnp.bfloat16)
    part_query = jnp.dot(lifted, w_query, preferred_element_type=jnp.float32)
    part_key = jnp.dot(lifted, key_projection_weight, preferred_element_type=jnp.float32)
    part_value = jnp.dot(lifted, value_projection_weight, preferred_element_type=jnp.float32)
    squares = jnp.sum(token_float * token_float, axis=1)
    sum_squares = lax.psum(squares, "seq")
    part_query, part_key, part_value = lax.psum((part_query, part_key, part_value), "seq")
    inv_rms = lax.rsqrt(sum_squares / model_width + norm_eps)
    query_vectors = apply_rotary(
        (part_query * inv_rms[:, None]).reshape(batch_rows, q_local, head_dim), positions
    ).astype(jnp.bfloat16)
    fresh_key_rows = apply_rotary(
        (part_key * inv_rms[:, None]).reshape(batch_rows, kv_local, head_dim), positions
    ).astype(jnp.bfloat16)
    fresh_value_rows = (
        (part_value * inv_rms[:, None]).reshape(batch_rows, kv_local, head_dim).astype(jnp.bfloat16)
    )
    grouped_queries = query_vectors.reshape(batch_rows, kv_local, query_group_count, head_dim)
    score_scale = head_dim ** (-0.5)
    scores = (
        jnp.einsum(
            "bhgd,bhtd->bhgt", grouped_queries, cache_keys, preferred_element_type=jnp.float32
        )
        * score_scale
    )
    slot_index = lax.axis_index("seq") * ctx_local + jnp.arange(ctx_local, dtype=jnp.int32)
    live_mask = slot_index[None, None, None, :] < lengths[:, None, None, None]
    local_max = jnp.max(jnp.where(live_mask, scores, masked_floor), axis=-1)
    weights = jnp.where(live_mask, jnp.exp(scores - local_max[..., None]), 0.0)
    local_sum = jnp.sum(weights, axis=-1)
    local_acc = jnp.einsum(
        "bhgt,bhtd->bhgd",
        weights.astype(jnp.bfloat16),
        stored_value_cache,
        preferred_element_type=jnp.float32,
    )
    merged_max, merged_sum, merged_acc = joined(
        (local_max, local_sum, local_acc), "seq", join_partial
    )
    score_new = (
        jnp.einsum(
            "bhgd,bhd->bhg", grouped_queries.astype(jnp.float32), fresh_key_rows.astype(jnp.float32)
        )
        * score_scale
    )
    row_max = jnp.maximum(merged_max, score_new)
    old_factor = jnp.exp(merged_max - row_max)
    new_weight = jnp.exp(score_new - row_max)
    total_weight = merged_sum * old_factor + new_weight
    attended = (
        merged_acc * old_factor[..., None]
        + new_weight[..., None] * fresh_value_rows.astype(jnp.float32)[:, :, None, :]
    )
    attn_rows = (
        (attended / total_weight[..., None])
        .reshape(batch_rows, q_local * head_dim)
        .astype(jnp.bfloat16)
    )
    out_part = jnp.dot(attn_rows, w_attn_out, preferred_element_type=jnp.float32)
    summed = lax.psum(out_part, "head")
    mid_stream = (token_float + summed).astype(jnp.bfloat16)
    full_tokens = lax.all_gather(mid_stream, "seq", axis=1, tiled=True)
    full_float = full_tokens.astype(jnp.float32)
    inv_rms_two = lax.rsqrt(jnp.mean(full_float * full_float, axis=1) + norm_eps)
    lifted_two = (full_float * inv_rms_two[:, None] * mamba_gain[None, :]).astype(jnp.bfloat16)
    inner = jnp.dot(lifted_two, w_in[0], preferred_element_type=jnp.float32)
    gate_branch = jnp.dot(lifted_two, w_in[1], preferred_element_type=jnp.float32)
    window = jnp.concatenate([conv_state, inner[:, None, :]], axis=1)
    mixed = jnp.sum(window * conv_weight[None, :, :], axis=1) + conv_bias[None, :]
    activated = jax.nn.silu(mixed)
    proj_part = jnp.dot(activated.astype(jnp.bfloat16), w_xproj, preferred_element_type=jnp.float32)
    projected = lax.psum(proj_part, ("seq", "head"))
    rank_width = w_dt.shape[0]
    state_width = ssm_state.shape[1]
    dt_low = projected[:, :rank_width].astype(jnp.bfloat16)
    input_map = projected[:, rank_width : rank_width + state_width]
    output_map = projected[:, rank_width + state_width :]
    step_size = jax.nn.softplus(
        jnp.dot(dt_low, w_dt, preferred_element_type=jnp.float32) + dt_bias[None, :]
    )
    decay = jnp.exp(step_size[:, None, :] * (-jnp.exp(a_log))[None, :, :])
    new_state = decay * ssm_state + (step_size * activated)[:, None, :] * input_map[:, :, None]
    readout = jnp.sum(output_map[:, :, None] * new_state, axis=1) + skip_gain[None, :] * activated
    gated = (readout * jax.nn.silu(gate_branch)).astype(jnp.bfloat16)
    mamba_part = jnp.dot(gated, w_mamba_out, preferred_element_type=jnp.float32)
    share = lax.psum_scatter(
        mamba_part.astype(jnp.bfloat16), "seq", scatter_dimension=1, tiled=True
    ).astype(jnp.float32)
    share = lax.psum(share, "head")
    hidden_out = (mid_stream.astype(jnp.float32) + share).astype(jnp.bfloat16)
    return (hidden_out, new_state)


def solution(mesh):
    in_specs = (
        P(("rep", "sub"), "seq"),
        P("seq"),
        P("seq", "head"),
        P("seq", "head"),
        P("seq", "head"),
        P("head", "seq"),
        P(("rep", "sub"), "head", "seq", None),
        P(("rep", "sub"), "head", "seq", None),
        P(("rep", "sub")),
        P(("rep", "sub")),
        P(),
        P(None, None, ("seq", "head")),
        P(None, ("seq", "head")),
        P(("seq", "head")),
        P(("rep", "sub"), None, ("seq", "head")),
        P(("seq", "head"), None),
        P(None, ("seq", "head")),
        P(("seq", "head")),
        P(None, ("seq", "head")),
        P(("seq", "head")),
        P(("rep", "sub"), None, ("seq", "head")),
        P(("seq", "head"), None),
    )
    out_specs = (P(("rep", "sub"), "seq"), P(("rep", "sub"), None, ("seq", "head")))
    return jax.shard_map(local, mesh=mesh, in_specs=in_specs, out_specs=out_specs, check_vma=False)
```

profile of v0, /device:TPU:0, one launch (start us, length us, event | category | flops | bytes accessed | tf_op | source)
XLA Modules:
  0.0 205.1 jit_solution(17046458614477309599)
XLA Ops:
  7.3 3.6 %fusion.46 = f32[8,2048]{1,0:T(8,128)} fusion(bf16[1024,2048]{1,0:T(8,128)(2,1)} %param.26, bf16[8,1024]{1,0:T(8,128)(2,1)} %param.24, f32[1024]{0:T(1024)} %param.25), kind=kOutput, calls=%fused_computation.68 | convolution fusion | flops 33579008 | bytes 4280320 | tf_op jit(solution)/shard_map/dot_general | solution.py:86
  11.2 0.2 fusion.44
  11.4 0.2 fusion.42
  11.7 21.4 %all-reduce = (f32[8]{0:T(128)S(1)}, f32[8,512]{1,0:T(8,128)S(1)}, f32[8,512]{1,0:T(8,128)S(1)}) all-reduce(f32[8]{0:T(128)S(1)} %fusion.25, f32[8,512]{1,0:T(8,128)S(1)} %fusion.44, f32[8,512]{1,0:T(8,128)S(1)} %fusion.42), channel_id=1, replica_groups=mesh['rep'=2,'seq'=4,'head'=2,'sub'=2] {'seq'}, use_global_device_ids=true, to_apply=%region_2.0 | all-reduce | flops 8200 | bytes 65600 | tf_op jit(solution)/shard_map/psum | solution.py:90
  33.6 14.7 %all-reduce.3.cloned.1.call-done = f32[8,2048]{1,0:T(8,128)} async-done(((f32[8,2048]{1,0:T(8,128)}), f32[8,2048]{1,0:T(8,128)}) %all-reduce.3.cloned.1.call-update) | async-done | bytes 65552 | tf_op jit(solution)/shard_map/psum | solution.py:91
  48.3 1.1 multiply_bitcast_fusion
  49.5 3.6 %select_reduce_fusion = (f32[8,4,4]{2,1,0:T(4,128)S(1)}, f32[8,4,4,512]{3,2,1,0:T(4,128)S(1)}) fusion(pred[8,512]{1,0:T(8,128)(4,1)S(1)} %broadcast_compare_fusion, bf16[8,4,512,128]{3,2,1,0:T(8,128)(2,1)} %param.30, bf16[8,4,4,64]{3,2,1,0:T(4,128)(2,1)S(1)} %bitcast.72, bf16[8,4,4,64]{3,2,1,0:T(4,128)(2,1)S(1)} %bitcast.70), kind=kOutput, calls=%fused_computation.21 | convolution fusion | flops 17039232 | bytes 4493824 | tf_op jit(solution)/shard_map/bhgd,bhtd->bhgt/dot_general | solution.py:105
  53.1 13.1 %all-gather = f32[32,4,4]{2,1,0:T(4,128)S(1)} all-gather(f32[8,4,4]{2,1,0:T(4,128)S(1)} %get-tuple-element.94), channel_id=2, replica_groups=mesh['rep'=2,'seq'=4,'head'=2,'sub'=2] {'seq'}, dimensions={0}, use_global_device_ids=true | all-gather | bytes 2560 | tf_op jit(solution)/shard_map/all_gather | solution.py:13
  66.2 0.3 fusion.13
  66.5 13.2 %all-gather.1 = f32[32,4,4]{2,1,0:T(4,128)S(1)} all-gather(f32[8,4,4]{2,1,0:T(4,128)S(1)} %fusion.13), channel_id=3, replica_groups=mesh['rep'=2,'seq'=4,'head'=2,'sub'=2] {'seq'}, dimensions={0}, use_global_device_ids=true | all-gather | bytes 2560 | tf_op jit(solution)/shard_map/all_gather | solution.py:13
  79.7 0.7 fusion.17
  80.4 13.9 %all-gather.2 = f32[32,4,4,128]{3,2,1,0:T(4,128)S(1)} all-gather(f32[8,4,4,128]{3,2,1,0:T(4,128)S(1)} %fusion.17), channel_id=4, replica_groups=mesh['rep'=2,'seq'=4,'head'=2,'sub'=2] {'seq'}, dimensions={0}, use_global_device_ids=true | all-gather | bytes 327680 | tf_op jit(solution)/shard_map/all_gather | solution.py:13
  94.3 0.2 fusion.37
  94.8 0.2 copy.52
  95.0 0.2 copy.53
  95.2 1.5 while.14
  95.4 0.2 fusion.73
  95.9 0.2 fusion.73
  96.4 0.2 fusion.73
  97.0 0.2 fusion.23
  97.2 2.8 %fusion.59 = f32[8,1024]{1,0:T(8,128)S(1)} fusion(bf16[8,2048]{1,0:T(8,128)(2,1)S(1)} %convert_element_type.78, bf16[2048,1024]{1,0:T(8,128)(2,1)} %param.29), kind=kOutput, calls=%fused_computation.88 | convolution fusion | flops 33554432 | bytes 4259840 | tf_op jit(solution)/shard_map/dot_general | solution.py:143
  100.0 8.3 %psum.53 = f32[8,1024]{1,0:T(8,128)S(1)} all-reduce(f32[8,1024]{1,0:T(8,128)S(1)} %fusion.59), channel_id=1, replica_groups=mesh['rep'=2,'seq'=4,'head'=2,'sub'=2] {'head'}, use_global_device_ids=true, to_apply=%region_9.10 | all-reduce | flops 8192 | bytes 65536 | tf_op jit(solution)/shard_map/psum | solution.py:144
  108.4 13.1 %all_gather.27 = bf16[8,4096]{1,0:T(8,128)(2,1)S(1)} all-gather(bf16[8,1024]{1,0:T(8,128)(2,1)S(1)} %fusion.26), channel_id=1, replica_groups=mesh['rep'=2,'seq'=4,'head'=2,'sub'=2] {'seq'}, dimensions={1}, use_global_device_ids=true | all-gather | bytes 81920 | tf_op jit(solution)/shard_map/all_gather | solution.py:146
  121.8 4.7 %fusion.9 = f32[8,1,1024]{2,0,1:T(8,128)S(1)} fusion(bf16[2,4096,1024]{2,1,0:T(8,128)(2,1)} %param.35, bf16[8,4096]{1,0:T(8,128)(2,1)S(1)} %all_gather.27, f32[4096]{0:T(1024)S(1)} %copy-done.9, f32[8]{0:T(128)S(1)} %add_rsqrt_fusion), kind=kOutput, calls=%fused_computation.16 | convolution fusion | flops 67239936 | bytes 8503328 | tf_op jit(solution)/shard_map/dot_general | solution.py:150
  126.5 0.3 fusion.34
  126.8 35.1 %psum.54 = f32[8,288]{1,0:T(8,128)S(1)} all-reduce(f32[8,288]{1,0:T(8,128)S(1)} %fusion.34), channel_id=1, replica_groups=mesh['rep'=2,'seq'=4,'head'=2,'sub'=2] {'seq','head'}, use_global_device_ids=true, to_apply=%region_12.13 | all-reduce | flops 2304 | bytes 18432 | tf_op jit(solution)/shard_map/psum | solution.py:156
  162.0 0.2 fusion.54
  162.2 1.0 multiply_reduce_fusion
  163.2 8.7 %convolution_convert_fusion = bf16[8,4096]{1,0:T(8,128)(2,1)} fusion(bf16[1024,4096]{1,0:T(8,128)(2,1)} %param.45, bf16[2,4096,1024]{2,1,0:T(8,128)(2,1)} %param.35, f32[8,1024]{1,0:T(8,128)S(1)} %get-tuple-element.79, f32[1024]{0:T(1024)S(1)} %copy-done.14, bf16[8,4096]{1,0:T(8,128)(2,1)S(1)} %all_gather.27, f32[4096]{0:T(1024)S(1)} %copy-done.9, ...), kind=kOutput, calls=%fused_computation.14 | convolution fusion | flops 134488064 | bytes 16998432 | tf_op jit(solution)/shard_map/dot_general | solution.py:169
  172.0 16.6 %reduce-scatter.2.cloned.1.call-done = bf16[8,1024]{1,0:T(8,128)(2,1)} async-done(((bf16[8,4096]{1,0:T(8,128)(2,1)}), bf16[8,1024]{1,0:T(8,128)(2,1)}) %reduce-scatter.2.cloned.1.call-update) | async-done | bytes 16400 | tf_op jit(solution)/shard_map/reduce_scatter | solution.py:170
  188.6 9.0 %psum.55 = f32[8,1024]{1,0:T(8,128)S(1)} all-reduce(bf16[8,1024]{1,0:T(8,128)(2,1)} %reduce-scatter.2.cloned.1.call-done), channel_id=1, replica_groups=mesh['rep'=2,'seq'=4,'head'=2,'sub'=2] {'head'}, use_global_device_ids=true, to_apply=%region_15.16 | all-reduce | flops 8192 | bytes 49152 | tf_op jit(solution)/shard_map/psum | solution.py:173
  197.6 0.6 add_convert_fusion.1
  (81 shorter events, 2.6 us)
Async XLA Ops:
  7.2 4.0 %copy-start = (bf16[1024,512]{1,0:T(8,128)(2,1)S(1)}, bf16[1024,512]{1,0:T(8,128)(2,1)}, u32[]{:S(2)}) copy-start(bf16[1024,512]{1,0:T(8,128)(2,1)} %param.27) | copy-start | bytes 3145732
  7.2 3.8 %copy-start.6 = (bf16[8,1024]{1,0:T(8,128)(2,1)S(1)}, bf16[8,1024]{1,0:T(8,128)(2,1)}, u32[]{:S(2)}) copy-start(bf16[8,1024]{1,0:T(8,128)(2,1)} %param.24) | copy-start | bytes 49156
  7.2 4.0 %copy-start.10 = (f32[1024]{0:T(1024)S(1)}, f32[1024]{0:T(1024)}, u32[]{:S(2)}) copy-start(f32[1024]{0:T(1024)} %param.25) | copy-start | bytes 12292
  7.2 4.2 %copy-start.2 = (bf16[1024,512]{1,0:T(8,128)(2,1)S(1)}, bf16[1024,512]{1,0:T(8,128)(2,1)}, u32[]{:S(2)}) copy-start(bf16[1024,512]{1,0:T(8,128)(2,1)} %param.28) | copy-start | bytes 3145732
  7.2 4.5 %copy-start.16 = (s32[8]{0:T(128)S(1)}, s32[8]{0:T(128)}, u32[]{:S(2)}) copy-start(s32[8]{0:T(128)} %param.33) | copy-start | bytes 100
  7.2 26.0 %copy-start.8 = (f32[16,1024]{1,0:T(8,128)S(1)}, f32[16,1024]{1,0:T(8,128)}, u32[]{:S(2)}) copy-start(f32[16,1024]{1,0:T(8,128)} %param.42) | copy-start | bytes 196612
  7.2 26.0 %copy-start.15 = (s32[8]{0:T(128)S(1)}, s32[8]{0:T(128)}, u32[]{:S(2)}) copy-start(s32[8]{0:T(128)} %param.32) | copy-start | bytes 100
  7.2 41.0 %all-reduce.3.cloned.1.call-start = ((), (), s32[]{:S(2)}) async-start(), calls=%async_computation.1 | async-start | bytes 131072 | tf_op jit(solution)/shard_map/psum | solution.py:91
  11.0 177.7 %reduce-scatter.2.cloned.1.call-start = ((), (), s32[]{:S(2)}) async-start(), calls=%async_computation.2 | async-start | bytes 81920 | tf_op jit(solution)/shard_map/reduce_scatter | solution.py:170
  48.3 31.4 %copy-start.1 = (bf16[8,4,512,128]{3,2,1,0:T(8,128)(2,1)S(1)}, bf16[8,4,512,128]{3,2,1,0:T(8,128)(2,1)}, u32[]{:S(2)}) copy-start(bf16[8,4,512,128]{3,2,1,0:T(8,128)(2,1)} %param.31) | copy-start | bytes 12582916
  80.4 41.3 %copy-start.9 = (f32[4096]{0:T(1024)S(1)}, f32[4096]{0:T(1024)}, u32[]{:S(2)}) copy-start(f32[4096]{0:T(1024)} %param.34) | copy-start | bytes 49156
  121.7 4.8 %copy-start.7 = (f32[8,3,1024]{2,0,1:T(8,128)S(1)}, f32[8,3,1024]{2,0,1:T(8,128)}, u32[]{:S(2)}) copy-start(f32[8,3,1024]{2,0,1:T(8,128)} %param.38) | copy-start | bytes 294916
  121.7 4.8 %copy-start.12 = (f32[4,1024]{1,0:T(4,128)S(1)}, f32[4,1024]{1,0:T(4,128)}, u32[]{:S(2)}) copy-start(f32[4,1024]{1,0:T(4,128)} %param.36) | copy-start | bytes 49156
  121.7 4.8 %copy-start.3 = (bf16[1024,288]{0,1:T(8,128)(2,1)S(1)}, bf16[1024,288]{0,1:T(8,128)(2,1)}, u32[]{:S(2)}) copy-start(bf16[1024,288]{0,1:T(8,128)(2,1)} %param.39) | copy-start | bytes 1769476
  121.7 4.8 %copy-start.11 = (f32[1024]{0:T(1024)S(1)}, f32[1024]{0:T(1024)}, u32[]{:S(2)}) copy-start(f32[1024]{0:T(1024)} %param.37) | copy-start | bytes 12292
  121.7 40.2 %copy-start.5 = (bf16[256,1024]{1,0:T(8,128)(2,1)S(1)}, bf16[256,1024]{1,0:T(8,128)(2,1)}, u32[]{:S(2)}) copy-start(bf16[256,1024]{1,0:T(8,128)(2,1)} %param.40) | copy-start | bytes 1572868
  121.7 40.2 %copy-start.13 = (f32[1024]{0:T(1024)S(1)}, f32[1024]{0:T(1024)}, u32[]{:S(2)}) copy-start(f32[1024]{0:T(1024)} %param.41) | copy-start | bytes 12292
  121.7 40.4 %copy-start.4 = (f32[8,16,1024]{2,1,0:T(8,128)S(1)}, f32[8,16,1024]{2,1,0:T(8,128)}, u32[]{:S(2)}) copy-start(f32[8,16,1024]{2,1,0:T(8,128)} %param.44) | copy-start | bytes 1572868
  121.8 41.5 %copy-start.14 = (f32[1024]{0:T(1024)S(1)}, f32[1024]{0:T(1024)}, u32[]{:S(2)}) copy-start(f32[1024]{0:T(1024)} %param.43) | copy-start | bytes 12292
Sparse Core Ops, SparseCore 0:
  11.1 37.1 all-reduce.2
  172.1 16.4 reduce-scatter.1
where the time goes:
time: 205 us
  blocking collectives  127 us (62%)
  waiting for transfers between devices  31.3 us (15%)
  matrix products  25.4 us (12%)
  between operations  14.4 us (7%)
  other arithmetic  4.82 us (2%)
    all_gather x3, blocking collectives, joined(): pieces = jax.tree.map(lambda part: lax.all_gather(part, axis), value)  40.2 us
    psum x1, blocking collectives, local(): projected = lax.psum(proj_part, ('seq', 'head'))  35.1 us
    psum x1, blocking collectives, local(): sum_squares = lax.psum(squares, 'seq')  21.4 us
    reduce_scatter x1, waiting for transfers between devices, local(): lax.psum_scatter(mamba_part.astype(jnp.bfloat16), 'seq', scatter_dimensio...  16.6 us
    psum x1, waiting for transfers between devices, local(): lax.psum((part_query, part_key, part_value), 'seq')  14.7 us
    all_gather x1, blocking collectives, local(): full_tokens = lax.all_gather(mid_stream, 'seq', axis=1, tiled=True)  13.1 us
    psum x1, blocking collectives, local(): share = lax.psum(share, 'head')  8.99 us
    dot_general x1, matrix products, local(): mamba_part = jnp.dot(gated, w_mamba_out, preferred_element_type=jnp.float32)  8.73 us
  transfers between devices with their start and end apart: 2, of which 2 were waited for; matrix products, arithmetic and copies ran while one was open for 1% of the time, Pallas kernels for 0%

commit v1 on v0

--- a/solution.py
+++ b/solution.py
@@ -153,7 +153,8 @@
     mixed = jnp.sum(window * conv_weight[None, :, :], axis=1) + conv_bias[None, :]
     activated = jax.nn.silu(mixed)
     proj_part = jnp.dot(activated.astype(jnp.bfloat16), w_xproj, preferred_element_type=jnp.float32)
-    projected = lax.psum(proj_part, ("seq", "head"))
+    small = lax.psum(proj_part, axis_name="head")
+    projected = lax.psum(small, "seq")
     rank_width = w_dt.shape[0]
     state_width = ssm_state.shape[1]
     dt_low = projected[:, :rank_width].astype(jnp.bfloat16)

time: 205 us -> 196 us (0.956)
  blocking collectives: 127 us -> 117 us
    psum x1 -> x2, blocking collectives: 35.1 us -> 24.7 us  [the longest x1 17.6 us: local(): projected = lax.psum(small, 'seq')]
where the time goes in v1:
time: 196 us
  blocking collectives  117 us (60%)
  waiting for transfers between devices  32.3 us (16%)
  matrix products  25.4 us (13%)
  between operations  14.4 us (7%)
  other arithmetic  4.82 us (2%)
    all_gather x3, blocking collectives, joined(): pieces = jax.tree.map(lambda part: lax.all_gather(part, axis), value)  40.2 us
    psum x1, blocking collectives, local(): sum_squares = lax.psum(squares, 'seq')  21.4 us
    psum x1, blocking collectives, local(): projected = lax.psum(small, 'seq')  17.6 us
    reduce_scatter x1, waiting for transfers between devices, local(): lax.psum_scatter(mamba_part.astype(jnp.bfloat16), 'seq', scatter_dimensio...  17.6 us
    psum x1, waiting for transfers between devices, local(): lax.psum((part_query, part_key, part_value), 'seq')  14.7 us
    all_gather x1, blocking collectives, local(): full_tokens = lax.all_gather(mid_stream, 'seq', axis=1, tiled=True)  13.1 us
    psum x1, blocking collectives, local(): share = lax.psum(share, 'head')  8.93 us
    dot_general x1, matrix products, local(): mamba_part = jnp.dot(gated, w_mamba_out, preferred_element_type=jnp.float32)  8.73 us
  transfers between devices with their start and end apart: 2, of which 2 were waited for; matrix products, arithmetic and copies ran while one was open for 1% of the time, Pallas kernels for 0%

profile of v1, /device:TPU:0, one launch (start us, length us, event | category | flops | bytes accessed | tf_op | source)
XLA Modules:
  0.0 195.6 jit_solution(12998376942372014993)
XLA Ops:
  7.3 3.6 %fusion.46 = f32[8,2048]{1,0:T(8,128)} fusion(bf16[1024,2048]{1,0:T(8,128)(2,1)} %param.26, bf16[8,1024]{1,0:T(8,128)(2,1)} %param.24, f32[1024]{0:T(1024)} %param.25), kind=kOutput, calls=%fused_computation.68 | convolution fusion | flops 33579008 | bytes 4280320 | tf_op jit(solution)/shard_map/dot_general | solution.py:86
  11.2 0.2 fusion.44
  11.4 0.2 fusion.42
  11.7 21.4 %all-reduce = (f32[8]{0:T(128)S(1)}, f32[8,512]{1,0:T(8,128)S(1)}, f32[8,512]{1,0:T(8,128)S(1)}) all-reduce(f32[8]{0:T(128)S(1)} %fusion.25, f32[8,512]{1,0:T(8,128)S(1)} %fusion.44, f32[8,512]{1,0:T(8,128)S(1)} %fusion.42), channel_id=1, replica_groups=mesh['rep'=2,'seq'=4,'head'=2,'sub'=2] {'seq'}, use_global_device_ids=true, to_apply=%region_2.0 | all-reduce | flops 8200 | bytes 65600 | tf_op jit(solution)/shard_map/psum | solution.py:90
  33.6 14.7 %all-reduce.3.cloned.1.call-done = f32[8,2048]{1,0:T(8,128)} async-done(((f32[8,2048]{1,0:T(8,128)}), f32[8,2048]{1,0:T(8,128)}) %all-reduce.3.cloned.1.call-update) | async-done | bytes 65552 | tf_op jit(solution)/shard_map/psum | solution.py:91
  48.3 1.1 multiply_bitcast_fusion
  49.5 3.6 %select_reduce_fusion = (f32[8,4,4]{2,1,0:T(4,128)S(1)}, f32[8,4,4,512]{3,2,1,0:T(4,128)S(1)}) fusion(pred[8,512]{1,0:T(8,128)(4,1)S(1)} %broadcast_compare_fusion, bf16[8,4,512,128]{3,2,1,0:T(8,128)(2,1)} %param.30, bf16[8,4,4,64]{3,2,1,0:T(4,128)(2,1)S(1)} %bitcast.72, bf16[8,4,4,64]{3,2,1,0:T(4,128)(2,1)S(1)} %bitcast.70), kind=kOutput, calls=%fused_computation.21 | convolution fusion | flops 17039232 | bytes 4493824 | tf_op jit(solution)/shard_map/bhgd,bhtd->bhgt/dot_general | solution.py:105
  53.1 13.1 %all-gather = f32[32,4,4]{2,1,0:T(4,128)S(1)} all-gather(f32[8,4,4]{2,1,0:T(4,128)S(1)} %get-tuple-element.94), channel_id=2, replica_groups=mesh['rep'=2,'seq'=4,'head'=2,'sub'=2] {'seq'}, dimensions={0}, use_global_device_ids=true | all-gather | bytes 2560 | tf_op jit(solution)/shard_map/all_gather | solution.py:13
  66.2 0.3 fusion.13
  66.5 13.2 %all-gather.1 = f32[32,4,4]{2,1,0:T(4,128)S(1)} all-gather(f32[8,4,4]{2,1,0:T(4,128)S(1)} %fusion.13), channel_id=3, replica_groups=mesh['rep'=2,'seq'=4,'head'=2,'sub'=2] {'seq'}, dimensions={0}, use_global_device_ids=true | all-gather | bytes 2560 | tf_op jit(solution)/shard_map/all_gather | solution.py:13
  79.7 0.7 fusion.17
  80.4 13.9 %all-gather.2 = f32[32,4,4,128]{3,2,1,0:T(4,128)S(1)} all-gather(f32[8,4,4,128]{3,2,1,0:T(4,128)S(1)} %fusion.17), channel_id=4, replica_groups=mesh['rep'=2,'seq'=4,'head'=2,'sub'=2] {'seq'}, dimensions={0}, use_global_device_ids=true | all-gather | bytes 327680 | tf_op jit(solution)/shard_map/all_gather | solution.py:13
  94.3 0.2 fusion.37
  94.8 0.2 copy.52
  95.2 1.5 while.14
  95.4 0.2 fusion.73
  95.9 0.2 fusion.73
  96.4 0.2 fusion.73
  97.0 0.2 fusion.23
  97.2 2.8 %fusion.59 = f32[8,1024]{1,0:T(8,128)S(1)} fusion(bf16[8,2048]{1,0:T(8,128)(2,1)S(1)} %convert_element_type.78, bf16[2048,1024]{1,0:T(8,128)(2,1)} %param.29), kind=kOutput, calls=%fused_computation.88 | convolution fusion | flops 33554432 | bytes 4259840 | tf_op jit(solution)/shard_map/dot_general | solution.py:143
  100.0 8.3 %psum.60 = f32[8,1024]{1,0:T(8,128)S(1)} all-reduce(f32[8,1024]{1,0:T(8,128)S(1)} %fusion.59), channel_id=1, replica_groups=mesh['rep'=2,'seq'=4,'head'=2,'sub'=2] {'head'}, use_global_device_ids=true, to_apply=%region_9.10 | all-reduce | flops 8192 | bytes 65536 | tf_op jit(solution)/shard_map/psum | solution.py:144
  108.4 13.1 %all_gather.27 = bf16[8,4096]{1,0:T(8,128)(2,1)S(1)} all-gather(bf16[8,1024]{1,0:T(8,128)(2,1)S(1)} %fusion.26), channel_id=1, replica_groups=mesh['rep'=2,'seq'=4,'head'=2,'sub'=2] {'seq'}, dimensions={1}, use_global_device_ids=true | all-gather | bytes 81920 | tf_op jit(solution)/shard_map/all_gather | solution.py:146
  121.8 4.7 %fusion.9 = f32[8,1,1024]{2,0,1:T(8,128)S(1)} fusion(bf16[2,4096,1024]{2,1,0:T(8,128)(2,1)} %param.35, bf16[8,4096]{1,0:T(8,128)(2,1)S(1)} %all_gather.27, f32[4096]{0:T(1024)S(1)} %copy-done.9, f32[8]{0:T(128)S(1)} %add_rsqrt_fusion), kind=kOutput, calls=%fused_computation.16 | convolution fusion | flops 67239936 | bytes 8503328 | tf_op jit(solution)/shard_map/dot_general | solution.py:150
  126.5 0.3 fusion.34
  126.8 7.1 %psum.61 = f32[8,288]{1,0:T(8,128)S(1)} all-reduce(f32[8,288]{1,0:T(8,128)S(1)} %fusion.34), channel_id=1, replica_groups=mesh['rep'=2,'seq'=4,'head'=2,'sub'=2] {'head'}, use_global_device_ids=true, to_apply=%region_12.13 | all-reduce | flops 2304 | bytes 18432 | tf_op jit(solution)/shard_map/psum | solution.py:156
  133.9 17.6 %psum.62 = f32[8,288]{1,0:T(8,128)S(1)} all-reduce(f32[8,288]{1,0:T(8,128)S(1)} %psum.61), channel_id=1, replica_groups=mesh['rep'=2,'seq'=4,'head'=2,'sub'=2] {'seq'}, use_global_device_ids=true, to_apply=%region_13.14 | all-reduce | flops 2304 | bytes 18432 | tf_op jit(solution)/shard_map/psum | solution.py:157
  151.6 0.2 fusion.54
  151.8 1.0 multiply_reduce_fusion
  152.9 8.7 %convolution_convert_fusion = bf16[8,4096]{1,0:T(8,128)(2,1)} fusion(bf16[1024,4096]{1,0:T(8,128)(2,1)} %param.45, bf16[2,4096,1024]{2,1,0:T(8,128)(2,1)} %param.35, f32[8,1024]{1,0:T(8,128)S(1)} %get-tuple-element.79, f32[1024]{0:T(1024)S(1)} %copy-done.14, bf16[8,4096]{1,0:T(8,128)(2,1)S(1)} %all_gather.27, f32[4096]{0:T(1024)S(1)} %copy-done.9, ...), kind=kOutput, calls=%fused_computation.14 | convolution fusion | flops 134488064 | bytes 16998432 | tf_op jit(solution)/shard_map/dot_general | solution.py:170
  161.6 17.6 %reduce-scatter.2.cloned.1.call-done = bf16[8,1024]{1,0:T(8,128)(2,1)} async-done(((bf16[8,4096]{1,0:T(8,128)(2,1)}), bf16[8,1024]{1,0:T(8,128)(2,1)}) %reduce-scatter.2.cloned.1.call-update) | async-done | bytes 16400 | tf_op jit(solution)/shard_map/reduce_scatter | solution.py:171
  179.2 8.9 %psum.63 = f32[8,1024]{1,0:T(8,128)S(1)} all-reduce(bf16[8,1024]{1,0:T(8,128)(2,1)} %reduce-scatter.2.cloned.1.call-done), channel_id=1, replica_groups=mesh['rep'=2,'seq'=4,'head'=2,'sub'=2] {'head'}, use_global_device_ids=true, to_apply=%region_16.17 | all-reduce | flops 8192 | bytes 49152 | tf_op jit(solution)/shard_map/psum | solution.py:174
  188.1 0.6 add_convert_fusion.1
  (82 shorter events, 2.7 us)
Async XLA Ops:
  7.2 4.0 %copy-start = (bf16[1024,512]{1,0:T(8,128)(2,1)S(1)}, bf16[1024,512]{1,0:T(8,128)(2,1)}, u32[]{:S(2)}) copy-start(bf16[1024,512]{1,0:T(8,128)(2,1)} %param.27) | copy-start | bytes 3145732
  7.2 3.8 %copy-start.6 = (bf16[8,1024]{1,0:T(8,128)(2,1)S(1)}, bf16[8,1024]{1,0:T(8,128)(2,1)}, u32[]{:S(2)}) copy-start(bf16[8,1024]{1,0:T(8,128)(2,1)} %param.24) | copy-start | bytes 49156
  7.2 4.0 %copy-start.10 = (f32[1024]{0:T(1024)S(1)}, f32[1024]{0:T(1024)}, u32[]{:S(2)}) copy-start(f32[1024]{0:T(1024)} %param.25) | copy-start | bytes 12292
  7.2 4.2 %copy-start.2 = (bf16[1024,512]{1,0:T(8,128)(2,1)S(1)}, bf16[1024,512]{1,0:T(8,128)(2,1)}, u32[]{:S(2)}) copy-start(bf16[1024,512]{1,0:T(8,128)(2,1)} %param.28) | copy-start | bytes 3145732
  7.2 4.5 %copy-start.16 = (s32[8]{0:T(128)S(1)}, s32[8]{0:T(128)}, u32[]{:S(2)}) copy-start(s32[8]{0:T(128)} %param.33) | copy-start | bytes 100
  7.2 26.0 %copy-start.8 = (f32[16,1024]{1,0:T(8,128)S(1)}, f32[16,1024]{1,0:T(8,128)}, u32[]{:S(2)}) copy-start(f32[16,1024]{1,0:T(8,128)} %param.42) | copy-start | bytes 196612
  7.2 26.0 %copy-start.15 = (s32[8]{0:T(128)S(1)}, s32[8]{0:T(128)}, u32[]{:S(2)}) copy-start(s32[8]{0:T(128)} %param.32) | copy-start | bytes 100
  7.2 41.0 %all-reduce.3.cloned.1.call-start = ((), (), s32[]{:S(2)}) async-start(), calls=%async_computation.1 | async-start | bytes 131072 | tf_op jit(solution)/shard_map/psum | solution.py:91
  11.0 168.2 %reduce-scatter.2.cloned.1.call-start = ((), (), s32[]{:S(2)}) async-start(), calls=%async_computation.2 | async-start | bytes 81920 | tf_op jit(solution)/shard_map/reduce_scatter | solution.py:171
  48.3 31.4 %copy-start.1 = (bf16[8,4,512,128]{3,2,1,0:T(8,128)(2,1)S(1)}, bf16[8,4,512,128]{3,2,1,0:T(8,128)(2,1)}, u32[]{:S(2)}) copy-start(bf16[8,4,512,128]{3,2,1,0:T(8,128)(2,1)} %param.31) | copy-start | bytes 12582916
  80.4 41.3 %copy-start.9 = (f32[4096]{0:T(1024)S(1)}, f32[4096]{0:T(1024)}, u32[]{:S(2)}) copy-start(f32[4096]{0:T(1024)} %param.34) | copy-start | bytes 49156
  121.7 4.8 %copy-start.7 = (f32[8,3,1024]{2,0,1:T(8,128)S(1)}, f32[8,3,1024]{2,0,1:T(8,128)}, u32[]{:S(2)}) copy-start(f32[8,3,1024]{2,0,1:T(8,128)} %param.38) | copy-start | bytes 294916
  121.7 4.8 %copy-start.12 = (f32[4,1024]{1,0:T(4,128)S(1)}, f32[4,1024]{1,0:T(4,128)}, u32[]{:S(2)}) copy-start(f32[4,1024]{1,0:T(4,128)} %param.36) | copy-start | bytes 49156
  121.7 4.8 %copy-start.3 = (bf16[1024,288]{0,1:T(8,128)(2,1)S(1)}, bf16[1024,288]{0,1:T(8,128)(2,1)}, u32[]{:S(2)}) copy-start(bf16[1024,288]{0,1:T(8,128)(2,1)} %param.39) | copy-start | bytes 1769476
  121.7 4.8 %copy-start.11 = (f32[1024]{0:T(1024)S(1)}, f32[1024]{0:T(1024)}, u32[]{:S(2)}) copy-start(f32[1024]{0:T(1024)} %param.37) | copy-start | bytes 12292
  121.7 29.9 %copy-start.5 = (bf16[256,1024]{1,0:T(8,128)(2,1)S(1)}, bf16[256,1024]{1,0:T(8,128)(2,1)}, u32[]{:S(2)}) copy-start(bf16[256,1024]{1,0:T(8,128)(2,1)} %param.40) | copy-start | bytes 1572868
  121.7 29.9 %copy-start.13 = (f32[1024]{0:T(1024)S(1)}, f32[1024]{0:T(1024)}, u32[]{:S(2)}) copy-start(f32[1024]{0:T(1024)} %param.41) | copy-start | bytes 12292
  121.7 30.1 %copy-start.4 = (f32[8,16,1024]{2,1,0:T(8,128)S(1)}, f32[8,16,1024]{2,1,0:T(8,128)}, u32[]{:S(2)}) copy-start(f32[8,16,1024]{2,1,0:T(8,128)} %param.44) | copy-start | bytes 1572868
  121.8 31.1 %copy-start.14 = (f32[1024]{0:T(1024)S(1)}, f32[1024]{0:T(1024)}, u32[]{:S(2)}) copy-start(f32[1024]{0:T(1024)} %param.43) | copy-start | bytes 12292
Sparse Core Ops, SparseCore 0:
  11.1 37.1 all-reduce.2
  161.8 17.3 reduce-scatter.1
